TPU v7x, 32 devices: a whole 2x2x4 slice. The times are simulated.
32 devices in a mesh: pb: 2 (over x), ka: 16 (over z, y, core).
Axes of the slice: x: 2, y: 2, z: 4, core: 2. Of those that a mesh axis runs over, the one named last changes fastest.
Arguments:
- coupling: bfloat16 [2, 16, 32, 32, 384], P('pb', 'ka'), may hold values from -0.796875 to 0.796875
- phonon_occ: float32 [2, 16, 32, 12], P('pb', 'ka'), may hold values from 0.1 to 1
- band_window: int32 [2, 16, 32, 32], P('pb', 'ka'), may hold values 0 or 1
- pair_count: int32 [2, 16, 16], P('pb', 'ka'), may hold values from 0 to 2, as said below
- k_target: int32 [2, 16, 32], P('pb', 'ka'), may hold values from 0 to 127
- kq_source: int32 [2, 16, 32], P('pb', 'ka'), may hold values from 0 to 127
- velocity: float32 [3, 32, 2048], P(None, None, 'ka'), may hold values from -6 to 6
- lifetime: float32 [32, 2048], P(None, 'ka'), may hold values from 0.5 to 2
Outputs:
- deviation: float32 [3, 32, 2048], P(None, None, 'ka')
Inputs may be any that keep to these rules, and one draw needn't show every extreme that they name: pair_count[p, a, d] is the number of live tile slots among slots d * 2 to d * 2 + 1 of device (p, a); in every q-group p some owner d receives 2 live tiles from every source.
All inputs are finite; a program needn't handle non-finite values. No bound on the sum of `band_window` on one device may be relied on, other than what follows from the above.
Results may differ from a plain program's by a relative error of at most 0.012.
Values may be sent and summed in bfloat16 or wider, within the bound.
A program may use at most 64 MiB of HBM per device.

v0:
```python
import jax
import jax.numpy as jnp
from jax import lax
from jax.sharding import PartitionSpec as P

MODES = 12
TILE_SLOTS = 2
ITERS = 4


def tile_terms(weight, chosen):
    return jnp.einsum("tnm,dmt->dnt", weight, chosen, preferred_element_type=jnp.float32)


def shards(coupling, phonon_occ, band_window, pair_count, k_target, kq_source, velocity, lifetime):
    tile_count = coupling.shape[2]
    block_width = velocity.shape[2]
    directions = velocity.shape[0]
    band_count = velocity.shape[1]
    slot_live = (
        (jnp.arange(TILE_SLOTS)[None, :] < pair_count[0, 0][:, None])
        .reshape(tile_count)
        .astype(jnp.float32)
    )
    window = band_window[0, 0].astype(jnp.float32) * slot_live[:, None]
    widened = coupling[0, 0].astype(jnp.float32)
    squared = (widened * widened).reshape(tile_count, band_count, band_count, MODES)
    summed = jnp.sum(squared * phonon_occ[0, 0][:, None, None, :], axis=3)
    weight = (summed * window[:, :, None]).astype(jnp.bfloat16)
    targets = lax.all_to_all(k_target[0, 0], "ka", split_axis=0, concat_axis=0, tiled=True)
    onehot = (targets[:, None] == jnp.arange(block_width, dtype=jnp.int32)[None, :]).astype(
        jnp.float32
    )
    deviation = lifetime[None] * velocity
    for iteration in range(ITERS):
        rounded = deviation.astype(jnp.bfloat16)
        local_terms = tile_terms(weight, jnp.take(rounded, kq_source[0, 0], axis=2))
        contribution = lax.all_to_all(
            local_terms.astype(jnp.bfloat16), "ka", split_axis=2, concat_axis=2, tiled=True
        ).astype(local_terms.dtype)
        partial_value = jnp.dot(
            contribution.reshape(directions * band_count, tile_count),
            onehot,
            precision=lax.Precision.HIGHEST,
            preferred_element_type=jnp.float32,
        )
        partial_value = partial_value.reshape(directions, band_count, block_width)
        scattering = lax.psum(partial_value.astype(jnp.bfloat16), "pb").astype(jnp.float32)
        deviation = lifetime[None] * (velocity + scattering)
    return deviation


def solution(mesh):
    placed = (
        P("pb", "ka", None, None, None),
        P("pb", "ka", None, None),
        P("pb", "ka", None, None),
        P("pb", "ka", None),
        P("pb", "ka", None),
        P("pb", "ka", None),
        P(None, None, "ka"),
        P(None, "ka"),
    )
    return jax.shard_map(
        shards, mesh=mesh, in_specs=placed, out_specs=P(None, None, "ka"), check_vma=False
    )
```

profile of v0, /device:TPU:0, one launch (start us, length us, event | category | flops | bytes accessed | tf_op | source)
XLA Modules:
  0.0 100.8 jit_solution(7904888660373477923)
XLA Ops:
  0.0 0.5 broadcast.93
  0.5 1.3 %reduce.6 = s32[32]{0:T(128)S(1)} reduce(s32[1,1,32]{2,1,0:T(1,128)} %param.14, s32[]{:T(128)} %broadcast.93), dimensions={0,1}, to_apply=%param.14.reduce_sub_computation.3 | reduce | bytes 260 | tf_op args[4]
  1.9 0.7 all_to_all.19
  2.5 7.4 %all-to-all-start.1 = ((s32[16,2,1]{1,2,0:T(1,128)}), s32[16,2,1]{1,2,0:T(1,128)S(1)}, u32[]{:S(2)}, u32[]{:S(2)}) async-start(s32[16,2,1]{1,2,0:T(1,128)} %bitcast.6), calls=%async_computation.1 | async-start | bytes 16384 | tf_op jit(solution)/shard_map/all_to_all | solution.py:30
  10.0 0.7 compare_select_fusion
  10.6 0.7 compare_and_fusion
  11.3 1.3 %convert_multiply_fusion = f32[1,1,32,32,384]{4,3,2,1,0:T(8,128)S(1)} fusion(bf16[1,1,32,32,384]{4,3,2,1,0:T(8,128)(2,1)} %param.10), kind=kLoop, calls=%fused_computation.5 | loop fusion | flops 786432 | bytes 2359296 | tf_op jit(solution)/shard_map/mul | solution.py:27
  12.6 0.0 copy-start.2
  12.6 0.0 copy-start
  12.6 0.0 copy-start.1
  12.6 5.9 %copy.30 = f32[1,1,32,32,384]{3,2,4,1,0:T(8,128)} copy(f32[1,1,32,32,384]{4,3,2,1,0:T(8,128)S(1)} %convert_multiply_fusion) | data formatting | bytes 3145728 | tf_op jit(solution)/shard_map/mul | solution.py:27
  18.6 0.0 copy-done.3
  18.6 0.0 copy-done.4
  18.6 0.1 fusion.33
  18.7 0.1 reshape.74
  18.8 3.7 %multiply_reduce_fusion = f32[32,32,32]{1,0,2:T(8,128)S(1)} fusion(f32[32,32,32,12]{1,0,3,2:T(8,128)} %bitcast.43, f32[32,12]{0,1:T(8,128)S(1)} %bitcast.44), kind=kLoop, calls=%fused_computation.4 | loop fusion | flops 753664 | bytes 1705472 | tf_op jit(solution)/shard_map/reduce_sum | solution.py:28
  22.5 0.0 copy-done.2
  22.5 0.1 bitcast_multiply_fusion
  22.6 0.3 copy.31
  23.0 0.1 copy.29
  23.1 0.6 gather_fusion
  23.7 0.9 fusion
  24.7 0.0 all-to-all-done.1
  24.7 6.0 %all-to-all-start = ((bf16[3,32,32]{1,0,2:T(4,128)(2,1)}), bf16[3,32,32]{1,0,2:T(4,128)(2,1)S(1)}, u32[]{:S(2)}, u32[]{:S(2)}) async-start(bf16[3,32,32]{1,0,2:T(4,128)(2,1)} %fusion), calls=%async_computation | async-start | bytes 65536 | tf_op jit(solution)/shard_map/all_to_all | solution.py:38
  30.7 0.7 reduce.7
  31.4 0.1 eq.15
  31.5 5.9 %all-to-all-done = bf16[3,32,32]{1,0,2:T(4,128)(2,1)S(1)} async-done(((bf16[3,32,32]{1,0,2:T(4,128)(2,1)}), bf16[3,32,32]{1,0,2:T(4,128)(2,1)S(1)}, u32[]{:S(2)}, u32[]{:S(2)}) %all-to-all-start) | async-done | bytes 6176 | tf_op jit(solution)/shard_map/all_to_all | solution.py:38
  37.3 0.2 convolution_convert_fusion.7
  37.5 8.4 %psum.28 = bf16[3,32,128]{2,1,0:T(8,128)(2,1)S(1)} all-reduce(bf16[3,32,128]{2,1,0:T(8,128)(2,1)S(1)} %convolution_convert_fusion.7), channel_id=1, replica_groups=mesh['pb'=2,'ka'=16] {'pb'}, use_global_device_ids=true, to_apply=%region_1.0 | all-reduce | flops 12288 | bytes 49152 | tf_op jit(solution)/shard_map/psum | solution.py:48
  45.9 0.1 copy.34
  46.0 0.6 gather_fusion.1
  46.6 0.3 fusion.1
  47.0 9.2 %all_to_all.29 = bf16[3,32,32]{1,0,2:T(4,128)(2,1)S(1)} all-to-all(bf16[3,32,32]{1,0,2:T(4,128)(2,1)S(1)} %fusion.1), channel_id=1, replica_groups=mesh['pb'=2,'ka'=16] {'ka'}, dimensions={2} | all-to-all | bytes 12288 | tf_op jit(solution)/shard_map/all_to_all | solution.py:38
  56.2 0.2 convolution_convert_fusion.6
  56.3 7.3 %psum.29 = bf16[3,32,128]{2,1,0:T(8,128)(2,1)S(1)} all-reduce(bf16[3,32,128]{2,1,0:T(8,128)(2,1)S(1)} %convolution_convert_fusion.6), channel_id=1, replica_groups=mesh['pb'=2,'ka'=16] {'pb'}, use_global_device_ids=true, to_apply=%region_2.4 | all-reduce | flops 12288 | bytes 49152 | tf_op jit(solution)/shard_map/psum | solution.py:48
  63.6 0.1 copy.37
  63.8 0.6 gather_fusion.2
  64.4 0.3 fusion.2
  64.7 9.2 %all_to_all.30 = bf16[3,32,32]{1,0,2:T(4,128)(2,1)S(1)} all-to-all(bf16[3,32,32]{1,0,2:T(4,128)(2,1)S(1)} %fusion.2), channel_id=1, replica_groups=mesh['pb'=2,'ka'=16] {'ka'}, dimensions={2} | all-to-all | bytes 12288 | tf_op jit(solution)/shard_map/all_to_all | solution.py:38
  73.9 0.2 convolution_convert_fusion.5
  74.1 8.5 %psum.30 = bf16[3,32,128]{2,1,0:T(8,128)(2,1)S(1)} all-reduce(bf16[3,32,128]{2,1,0:T(8,128)(2,1)S(1)} %convolution_convert_fusion.5), channel_id=1, replica_groups=mesh['pb'=2,'ka'=16] {'pb'}, use_global_device_ids=true, to_apply=%region_3.5 | all-reduce | flops 12288 | bytes 49152 | tf_op jit(solution)/shard_map/psum | solution.py:48
  82.5 0.1 copy.40
  82.7 0.6 gather_fusion.3
  83.3 0.3 fusion.3
  83.6 9.2 %all_to_all.31 = bf16[3,32,32]{1,0,2:T(4,128)(2,1)S(1)} all-to-all(bf16[3,32,32]{1,0,2:T(4,128)(2,1)S(1)} %fusion.3), channel_id=1, replica_groups=mesh['pb'=2,'ka'=16] {'ka'}, dimensions={2} | all-to-all | bytes 12288 | tf_op jit(solution)/shard_map/all_to_all | solution.py:38
  92.8 0.2 convolution_convert_fusion.4
  93.0 7.1 %psum.31 = bf16[3,32,128]{2,1,0:T(8,128)(2,1)S(1)} all-reduce(bf16[3,32,128]{2,1,0:T(8,128)(2,1)S(1)} %convolution_convert_fusion.4), channel_id=1, replica_groups=mesh['pb'=2,'ka'=16] {'pb'}, use_global_device_ids=true, to_apply=%region_4.6 | all-reduce | flops 12288 | bytes 49152 | tf_op jit(solution)/shard_map/psum | solution.py:48
  100.1 0.6 add_multiply_fusion
  (11 shorter events, 0.1 us)
Async XLA Ops:
  0.0 18.6 %copy-start.3 = (f32[1,1,32,12]{2,1,3,0:T(1,128)S(1)}, f32[1,1,32,12]{2,1,3,0:T(1,128)}, u32[]{:S(2)}) copy-start(f32[1,1,32,12]{2,1,3,0:T(1,128)} %param.11) | copy-start | bytes 4612
  0.0 18.6 %copy-start.4 = (s32[1,1,16]{2,1,0:T(1,128)S(1)}, s32[1,1,16]{2,1,0:T(1,128)}, u32[]{:S(2)}) copy-start(s32[1,1,16]{2,1,0:T(1,128)} %param.13) | copy-start | bytes 196
  2.5 22.1 %all-to-all-start.1 = ((s32[16,2,1]{1,2,0:T(1,128)}), s32[16,2,1]{1,2,0:T(1,128)S(1)}, u32[]{:S(2)}, u32[]{:S(2)}) async-start(s32[16,2,1]{1,2,0:T(1,128)} %bitcast.6), calls=%async_computation.1 | async-start | bytes 16384 | tf_op jit(solution)/shard_map/all_to_all | solution.py:30
  12.6 9.9 %copy-start.2 = (s32[1,1,32,32]{3,2,1,0:T(8,128)S(1)}, s32[1,1,32,32]{3,2,1,0:T(8,128)}, u32[]{:S(2)}) copy-start(s32[1,1,32,32]{3,2,1,0:T(8,128)} %param.12) | copy-start | bytes 12292
  12.6 10.3 %copy-start = (f32[3,32,128]{2,1,0:T(8,128)S(1)}, f32[3,32,128]{2,1,0:T(8,128)}, u32[]{:S(2)}) copy-start(f32[3,32,128]{2,1,0:T(8,128)} %param.16) | copy-start | bytes 147460
  12.6 10.3 %copy-start.1 = (f32[32,128]{1,0:T(8,128)S(1)}, f32[32,128]{1,0:T(8,128)}, u32[]{:S(2)}) copy-start(f32[32,128]{1,0:T(8,128)} %param.17) | copy-start | bytes 49156
  24.7 12.6 %all-to-all-start = ((bf16[3,32,32]{1,0,2:T(4,128)(2,1)}), bf16[3,32,32]{1,0,2:T(4,128)(2,1)S(1)}, u32[]{:S(2)}, u32[]{:S(2)}) async-start(bf16[3,32,32]{1,0,2:T(4,128)(2,1)} %fusion), calls=%async_computation | async-start | bytes 65536 | tf_op jit(solution)/shard_map/all_to_all | solution.py:38
where the time goes:
time: 101 us
  blocking collectives  58.8 us (58%)
  starting transfers between devices  13.4 us (13%)
  local copies, waits for them, and re-layouts  10.7 us (11%)
  other arithmetic  9.2 us (9%)
  waiting for transfers between devices  5.88 us (6%)
  matrix products  2.6 us (3%)
    psum x4, blocking collectives, shards(): lax.psum(partial_value.astype(jnp.bfloat16), 'pb').astype(jnp.float32)  31.2 us
    all_to_all x3, blocking collectives, shards(): lax.all_to_all(local_terms.astype(jnp.bfloat16), 'ka', split_axis=2, conc...  27.6 us
    all_to_all x1, starting transfers between devices, shards(): lax.all_to_all(k_target[0, 0], 'ka', split_axis=0, concat_axis=0, tiled=T...  7.41 us
    all_to_all x1, starting transfers between devices, shards(): lax.all_to_all(local_terms.astype(jnp.bfloat16), 'ka', split_axis=2, conc...  6.01 us
    mul x1, local copies, waits for them, and re-layouts, shards(): widened * widened  5.94 us
    all_to_all x1, waiting for transfers between devices, shards(): lax.all_to_all(local_terms.astype(jnp.bfloat16), 'ka', split_axis=2, conc...  5.88 us
    reduce_sum x1, other arithmetic, shards(): summed = jnp.sum(squared * phonon_occ[0, 0][:, None, None, :], axis=3)  3.71 us
    gather x4, local copies, waits for them, and re-layouts, shards(): local_terms = tile_terms(weight, jnp.take(rounded, kq_source[0, 0], axis=2))  2.44 us
  transfers between devices with their start and end apart: 2, of which 1 were waited for; matrix products, arithmetic and copies ran while one was open for 15% of the time, Pallas kernels for 0%

commit v1 on v0

--- a/solution.py
+++ b/solution.py
@@ -35,8 +35,14 @@
     for iteration in range(ITERS):
         rounded = deviation.astype(jnp.bfloat16)
         local_terms = tile_terms(weight, jnp.take(rounded, kq_source[0, 0], axis=2))
-        contribution = lax.all_to_all(
-            local_terms.astype(jnp.bfloat16), "ka", split_axis=2, concat_axis=2, tiled=True
+        contribution = jnp.concatenate(
+            lax.all_to_all(
+                jnp.stack(jnp.split(local_terms.astype(jnp.bfloat16), lax.axis_size("ka"), axis=2)),
+                "ka",
+                0,
+                0,
+            ),
+            axis=2,
         ).astype(local_terms.dtype)
         partial_value = jnp.dot(
             contribution.reshape(directions * band_count, tile_count),

time: 101 us -> 102 us (level)
  local copies, waits for them, and re-layouts: 10.7 us -> 12.2 us
where the time goes in v1:
time: 102 us
  blocking collectives  58.6 us (57%)
  starting transfers between devices  13.4 us (13%)
  local copies, waits for them, and re-layouts  12.2 us (12%)
  other arithmetic  9.2 us (9%)
  waiting for transfers between devices  5.82 us (6%)
  matrix products  1.99 us (2%)
    psum x4, blocking collectives, shards(): lax.psum(partial_value.astype(jnp.bfloat16), 'pb').astype(jnp.float32)  31.2 us
    all_to_all x3, blocking collectives, shards(): lax.all_to_all(jnp.stack(jnp.split(local_terms.astype(jnp.bfloat16), lax....  27.4 us
    all_to_all x1, starting transfers between devices, shards(): lax.all_to_all(k_target[0, 0], 'ka', split_axis=0, concat_axis=0, tiled=T...  7.41 us
    all_to_all x1, starting transfers between devices, shards(): lax.all_to_all(jnp.stack(jnp.split(local_terms.astype(jnp.bfloat16), lax....  6.01 us
    mul x1, local copies, waits for them, and re-layouts, shards(): widened * widened  5.94 us
    all_to_all x1, waiting for transfers between devices, shards(): lax.all_to_all(jnp.stack(jnp.split(local_terms.astype(jnp.bfloat16), lax....  5.81 us
    reduce_sum x1, other arithmetic, shards(): summed = jnp.sum(squared * phonon_occ[0, 0][:, None, None, :], axis=3)  3.71 us
    gather x4, local copies, waits for them, and re-layouts, shards(): local_terms = tile_terms(weight, jnp.take(rounded, kq_source[0, 0], axis=2))  2.44 us
  transfers between devices with their start and end apart: 2, of which 1 were waited for; matrix products, arithmetic and copies ran while one was open for 15% of the time, Pallas kernels for 0%

profile of v1, /device:TPU:0, one launch (start us, length us, event | category | flops | bytes accessed | tf_op | source)
XLA Modules:
  0.0 101.5 jit_solution(10398023093548167024)
XLA Ops:
  0.0 0.5 broadcast.93
  0.5 1.3 %reduce.6 = s32[32]{0:T(128)S(1)} reduce(s32[1,1,32]{2,1,0:T(1,128)} %param.14, s32[]{:T(128)} %broadcast.93), dimensions={0,1}, to_apply=%param.14.reduce_sub_computation.3 | reduce | bytes 260 | tf_op args[4]
  1.9 0.7 all_to_all.19
  2.5 7.4 %all-to-all-start.1 = ((s32[16,2,1]{1,2,0:T(1,128)}), s32[16,2,1]{1,2,0:T(1,128)S(1)}, u32[]{:S(2)}, u32[]{:S(2)}) async-start(s32[16,2,1]{1,2,0:T(1,128)} %bitcast.24), calls=%async_computation.1 | async-start | bytes 16384 | tf_op jit(solution)/shard_map/all_to_all | solution.py:30
  10.0 0.7 compare_select_fusion
  10.6 0.7 compare_and_fusion
  11.3 1.3 %convert_multiply_fusion = f32[1,1,32,32,384]{4,3,2,1,0:T(8,128)S(1)} fusion(bf16[1,1,32,32,384]{4,3,2,1,0:T(8,128)(2,1)} %param.10), kind=kLoop, calls=%fused_computation.5 | loop fusion | flops 786432 | bytes 2359296 | tf_op jit(solution)/shard_map/mul | solution.py:27
  12.6 0.0 copy-start.2
  12.6 0.0 copy-start
  12.6 0.0 copy-start.1
  12.6 5.9 %copy.62 = f32[1,1,32,32,384]{3,2,4,1,0:T(8,128)} copy(f32[1,1,32,32,384]{4,3,2,1,0:T(8,128)S(1)} %convert_multiply_fusion) | data formatting | bytes 3145728 | tf_op jit(solution)/shard_map/mul | solution.py:27
  18.6 0.0 copy-done.4
  18.6 0.1 fusion.29
  18.7 0.1 reshape.98
  18.8 3.7 %multiply_reduce_fusion = f32[32,32,32]{1,0,2:T(8,128)S(1)} fusion(f32[32,32,32,12]{1,0,3,2:T(8,128)} %bitcast.311, f32[32,12]{0,1:T(8,128)S(1)} %bitcast.316), kind=kLoop, calls=%fused_computation.4 | loop fusion | flops 753664 | bytes 1705472 | tf_op jit(solution)/shard_map/reduce_sum | solution.py:28
  22.5 0.0 copy-done.2
  22.5 0.1 bitcast_multiply_fusion
  22.6 0.3 copy.63
  23.0 0.1 copy.61
  23.1 0.6 gather_fusion
  23.7 0.3 fusion
  24.3 0.6 copy.64
  24.9 0.0 all-to-all-done.1
  24.9 6.0 %all-to-all-start = ((bf16[16,3,32,2]{2,3,1,0:T(2,128)(2,1)}), bf16[16,3,32,2]{2,3,1,0:T(2,128)(2,1)S(1)}, u32[]{:S(2)}, u32[]{:S(2)}) async-start(bf16[16,3,32,2]{2,3,1,0:T(2,128)(2,1)} %copy.64), calls=%async_computation | async-start | bytes 49152 | tf_op jit(solution)/shard_map/all_to_all | solution.py:39
  30.9 0.7 reduce.7
  31.6 0.1 eq.15
  31.7 5.8 %all-to-all-done = bf16[16,3,32,2]{2,3,1,0:T(2,128)(2,1)S(1)} async-done(((bf16[16,3,32,2]{2,3,1,0:T(2,128)(2,1)}), bf16[16,3,32,2]{2,3,1,0:T(2,128)(2,1)S(1)}, u32[]{:S(2)}, u32[]{:S(2)}) %all-to-all-start) | async-done | bytes 6176 | tf_op jit(solution)/shard_map/all_to_all | solution.py:39
  37.5 0.2 convolution_convert_fusion.7
  37.7 8.3 %psum.28 = bf16[3,32,128]{2,1,0:T(8,128)(2,1)S(1)} all-reduce(bf16[3,32,128]{2,1,0:T(8,128)(2,1)S(1)} %convolution_convert_fusion.7), channel_id=1, replica_groups=mesh['pb'=2,'ka'=16] {'pb'}, use_global_device_ids=true, to_apply=%region_1.0 | all-reduce | flops 12288 | bytes 49152 | tf_op jit(solution)/shard_map/psum | solution.py:54
  46.0 0.1 copy.68
  46.2 0.6 gather_fusion.1
  46.8 0.3 fusion.1
  47.3 9.1 %all_to_all.29 = bf16[16,3,32,2]{2,3,1,0:T(2,128)(2,1)S(1)} all-to-all(bf16[16,3,32,2]{2,3,1,0:T(2,128)(2,1)S(1)} %copy.70), channel_id=1, replica_groups=mesh['pb'=2,'ka'=16] {'ka'}, dimensions={0} | all-to-all | bytes 12288 | tf_op jit(solution)/shard_map/all_to_all | solution.py:39
  56.5 0.2 convolution_convert_fusion.6
  56.7 7.3 %psum.29 = bf16[3,32,128]{2,1,0:T(8,128)(2,1)S(1)} all-reduce(bf16[3,32,128]{2,1,0:T(8,128)(2,1)S(1)} %convolution_convert_fusion.6), channel_id=1, replica_groups=mesh['pb'=2,'ka'=16] {'pb'}, use_global_device_ids=true, to_apply=%region_2.4 | all-reduce | flops 12288 | bytes 49152 | tf_op jit(solution)/shard_map/psum | solution.py:54
  64.0 0.1 copy.73
  64.1 0.6 gather_fusion.2
  64.7 0.3 fusion.2
  65.3 9.1 %all_to_all.30 = bf16[16,3,32,2]{2,3,1,0:T(2,128)(2,1)S(1)} all-to-all(bf16[16,3,32,2]{2,3,1,0:T(2,128)(2,1)S(1)} %copy.75), channel_id=1, replica_groups=mesh['pb'=2,'ka'=16] {'ka'}, dimensions={0} | all-to-all | bytes 12288 | tf_op jit(solution)/shard_map/all_to_all | solution.py:39
  74.4 0.2 convolution_convert_fusion.5
  74.6 8.5 %psum.30 = bf16[3,32,128]{2,1,0:T(8,128)(2,1)S(1)} all-reduce(bf16[3,32,128]{2,1,0:T(8,128)(2,1)S(1)} %convolution_convert_fusion.5), channel_id=1, replica_groups=mesh['pb'=2,'ka'=16] {'pb'}, use_global_device_ids=true, to_apply=%region_3.5 | all-reduce | flops 12288 | bytes 49152 | tf_op jit(solution)/shard_map/psum | solution.py:54
  83.1 0.1 copy.78
  83.3 0.6 gather_fusion.3
  83.9 0.3 fusion.3
  84.4 9.1 %all_to_all.31 = bf16[16,3,32,2]{2,3,1,0:T(2,128)(2,1)S(1)} all-to-all(bf16[16,3,32,2]{2,3,1,0:T(2,128)(2,1)S(1)} %copy.80), channel_id=1, replica_groups=mesh['pb'=2,'ka'=16] {'ka'}, dimensions={0} | all-to-all | bytes 12288 | tf_op jit(solution)/shard_map/all_to_all | solution.py:39
  93.6 0.2 convolution_convert_fusion.4
  93.8 7.1 %psum.31 = bf16[3,32,128]{2,1,0:T(8,128)(2,1)S(1)} all-reduce(bf16[3,32,128]{2,1,0:T(8,128)(2,1)S(1)} %convolution_convert_fusion.4), channel_id=1, replica_groups=mesh['pb'=2,'ka'=16] {'pb'}, use_global_device_ids=true, to_apply=%region_4.6 | all-reduce | flops 12288 | bytes 49152 | tf_op jit(solution)/shard_map/psum | solution.py:54
  100.9 0.6 add_multiply_fusion
  (83 shorter events, 0.9 us)
Async XLA Ops:
  0.0 18.6 %copy-start.3 = (f32[1,1,32,12]{2,1,3,0:T(1,128)S(1)}, f32[1,1,32,12]{2,1,3,0:T(1,128)}, u32[]{:S(2)}) copy-start(f32[1,1,32,12]{2,1,3,0:T(1,128)} %param.11) | copy-start | bytes 4612
  0.0 18.6 %copy-start.4 = (s32[1,1,16]{2,1,0:T(1,128)S(1)}, s32[1,1,16]{2,1,0:T(1,128)}, u32[]{:S(2)}) copy-start(s32[1,1,16]{2,1,0:T(1,128)} %param.13) | copy-start | bytes 196
  2.5 22.4 %all-to-all-start.1 = ((s32[16,2,1]{1,2,0:T(1,128)}), s32[16,2,1]{1,2,0:T(1,128)S(1)}, u32[]{:S(2)}, u32[]{:S(2)}) async-start(s32[16,2,1]{1,2,0:T(1,128)} %bitcast.24), calls=%async_computation.1 | async-start | bytes 16384 | tf_op jit(solution)/shard_map/all_to_all | solution.py:30
  12.6 9.9 %copy-start.2 = (s32[1,1,32,32]{3,2,1,0:T(8,128)S(1)}, s32[1,1,32,32]{3,2,1,0:T(8,128)}, u32[]{:S(2)}) copy-start(s32[1,1,32,32]{3,2,1,0:T(8,128)} %param.12) | copy-start | bytes 12292
  12.6 10.3 %copy-start = (f32[3,32,128]{2,1,0:T(8,128)S(1)}, f32[3,32,128]{2,1,0:T(8,128)}, u32[]{:S(2)}) copy-start(f32[3,32,128]{2,1,0:T(8,128)} %param.16) | copy-start | bytes 147460
  12.6 10.3 %copy-start.1 = (f32[32,128]{1,0:T(8,128)S(1)}, f32[32,128]{1,0:T(8,128)}, u32[]{:S(2)}) copy-start(f32[32,128]{1,0:T(8,128)} %param.17) | copy-start | bytes 49156
  24.9 12.6 %all-to-all-start = ((bf16[16,3,32,2]{2,3,1,0:T(2,128)(2,1)}), bf16[16,3,32,2]{2,3,1,0:T(2,128)(2,1)S(1)}, u32[]{:S(2)}, u32[]{:S(2)}) async-start(bf16[16,3,32,2]{2,3,1,0:T(2,128)(2,1)} %copy.64), calls=%async_computation | async-start | bytes 49152 | tf_op jit(solution)/shard_map/all_to_all | solution.py:39
